TPU v7x, 32 devices: a whole 2x2x4 slice. The times are simulated.
32 devices in a mesh: px: 2 (over core), py: 4 (over z), ta: 4 (over y, x).
Axes of the slice: x: 2, y: 2, z: 4, core: 2. Of those that a mesh axis runs over, the one named last changes fastest.
Arguments:
- snapshots: bfloat16 [384, 5, 65536], P('ta', None, ('px', 'py')), may hold values from -6 to 6
- quad_weights: float32 [65536], P(('px', 'py')), may hold values from 1 to 10
- spectral_indices: int32 [32], replicated, may hold values from 0 to 127
Outputs:
- spectra: float32 [32, 2, 2, 5, 65536], P('ta', None, None, None, ('px', 'py'))
- gram: float32 [32, 2, 2, 2], P('ta')
All inputs are finite; a program needn't handle non-finite values.
Results may differ from a plain program's by a relative error of at most 0.0042.
Values may be sent and summed in bfloat16 or wider, within the bound.
A program may use at most 128 MiB of HBM per device.

v0:
```python
import math
import jax
import jax.numpy as jnp
from jax import lax
from jax.sharding import PartitionSpec as P

VARS = 5
BLK = 256
HOP = 128
SEGMENT_NUMBER = 2
RETAINED_MODES = 32


def make_rotation_multipliers(spectral_indices, temporal_locations):
    segment_beginnings = jnp.arange(SEGMENT_NUMBER, dtype=jnp.int32) * HOP
    segment_shifts = temporal_locations[None, :] - segment_beginnings[:, None]
    inside = (segment_shifts >= 0) & (segment_shifts < BLK)
    window = 0.5 - 0.5 * jnp.cos(2.0 * math.pi * segment_shifts.astype(jnp.float32) / BLK)
    window = jnp.where(inside, window, jnp.float32(0.0)) / jnp.sqrt(jnp.float32(3.0 * BLK / 8.0))
    phases = jnp.mod(spectral_indices[:, None, None] * segment_shifts[None, :, :], BLK)
    angles = 2.0 * math.pi * phases.astype(jnp.float32) / BLK
    real_part = jnp.cos(angles) * window[None]
    imag_part = -jnp.sin(angles) * window[None]
    gathered_segments = jnp.stack([real_part, imag_part], axis=2)
    return gathered_segments.reshape(
        RETAINED_MODES * SEGMENT_NUMBER * 2, temporal_locations.shape[0]
    ).astype(jnp.bfloat16)


def gram_terms(spectra):
    flat = spectra.reshape(spectra.shape[0], 2 * SEGMENT_NUMBER, -1)
    inner = jnp.einsum("fam,fbm->fab", flat, flat, precision=lax.Precision.HIGHEST)
    inner = inner.reshape(spectra.shape[0], SEGMENT_NUMBER, 2, SEGMENT_NUMBER, 2)
    real_part = inner[:, :, 0, :, 0] + inner[:, :, 1, :, 1]
    imag_part = inner[:, :, 0, :, 1] - inner[:, :, 1, :, 0]
    return jnp.stack([real_part, imag_part], axis=-1)


def on_device(snapshots, quad_weights, spectral_indices):
    record_length = snapshots.shape[0]
    point_count = snapshots.shape[2]
    groups = lax.axis_size("ta")
    temporal_locations = lax.axis_index("ta") * record_length + jnp.arange(
        record_length, dtype=jnp.int32
    )
    rotation_multipliers = make_rotation_multipliers(spectral_indices, temporal_locations)
    flat_snapshots = snapshots.reshape(record_length, VARS * point_count)
    raw = lax.psum_scatter(
        jnp.dot(rotation_multipliers, flat_snapshots, preferred_element_type=jnp.float32),
        "ta",
        scatter_dimension=0,
        tiled=True,
    )
    raw = raw.reshape(RETAINED_MODES // groups, SEGMENT_NUMBER, 2, VARS, point_count)
    spectra = raw * jnp.sqrt(quad_weights)
    summed = lax.psum(gram_terms(spectra), ("px", "py"))
    total_points = point_count * lax.axis_size("px") * lax.axis_size("py")
    gram = summed / jnp.float32(total_points * VARS)
    return (spectra, gram)


def solution(mesh):
    return jax.shard_map(
        on_device,
        mesh=mesh,
        in_specs=(P("ta", None, ("px", "py")), P(("px", "py")), P()),
        out_specs=(P("ta", None, None, None, ("px", "py")), P("ta", None, None, None)),
        check_vma=False,
    )
```

profile of v0, /device:TPU:1, one launch (start us, length us, event | category | flops | bytes accessed | tf_op | source)
XLA Modules:
  0.0 306.7 jit_solution(16101970219021868528)
XLA Ops:
  7.2 0.0 reduce-scatter.2.cloned.1.call-start
  7.2 0.1 broadcast_subtract_fusion
  7.3 0.1 fusion.6
  7.4 0.9 multiply_convert_fusion.1
  8.4 12.7 %copy.17 = bf16[96,5,8192]{0,2,1:T(8,128)(2,1)} copy(bf16[96,5,8192]{2,0,1:T(8,128)(2,1)} %param.3) | data formatting | bytes 15728640 | tf_op args[0]
  21.1 13.8 %fusion.7 = f32[128,40960]{1,0:T(8,128)} fusion(bf16[128,96]{1,0:T(8,128)(2,1)S(1)} %bitcast.8, bf16[96,40960]{0,1:T(8,128)(2,1)} %bitcast.7), kind=kOutput, calls=%fused_computation.24 | convolution fusion | flops 1006632960 | bytes 28860416 | tf_op jit(solution)/shard_map/dot_general | solution.py:49
  34.9 0.0 copy-start
  34.9 0.0 reduce-scatter.2.cloned.1.call-update
  35.0 0.7 copy-done
  35.7 0.1 mul.103
  35.8 188.9 %reduce-scatter.2.cloned.1.call-done = f32[32,40960]{1,0:T(8,128)} async-done(((f32[128,40960]{1,0:T(8,128)}), f32[32,40960]{1,0:T(8,128)}) %reduce-scatter.2.cloned.1.call-update) | async-done | bytes 5242896 | tf_op jit(solution)/shard_map/reduce_scatter | solution.py:48
  224.8 5.8 %reshape.194 = f32[8,4,40960]{2,1,0:T(4,128)} reshape(f32[32,40960]{1,0:T(8,128)} %reduce-scatter.2.cloned.1.call-done) | data formatting | bytes 10485760 | tf_op jit(solution)/shard_map/reshape | solution.py:54
  230.6 25.9 %fusion = f32[8,4,4]{2,1,0:T(4,128)S(1)} fusion(f32[8,4,40960]{2,1,0:T(4,128)} %reshape.194, f32[40960]{0:T(1024)S(1)} %mul.103), kind=kOutput, calls=%fused_computation | convolution fusion | flops 64225280 | bytes 5407232 | tf_op jit(solution)/shard_map/fam,fbm->fab/dot_general | solution.py:32
  256.5 0.1 copy.18
  256.7 17.6 %psum.7 = f32[8,2,2,2]{0,2,3,1:T(2,128)S(1)} all-reduce(f32[8,2,2,2]{0,2,3,1:T(2,128)S(1)} %pad_maximum_fusion.1), channel_id=1, replica_groups=mesh['px'=2,'py'=4,'ta'=4] {'px','py'}, use_global_device_ids=true, to_apply=%region_1.2 | all-reduce | flops 64 | bytes 512 | tf_op jit(solution)/shard_map/psum | solution.py:56
  274.3 0.6 copy.20
  274.9 7.3 %reshape.193 = f32[8,2,2,5,8192]{4,3,2,1,0:T(8,128)} reshape(f32[32,40960]{1,0:T(8,128)} %reduce-scatter.2.cloned.1.call-done) | data formatting | bytes 10485760 | tf_op jit(solution)/shard_map/reshape | solution.py:54
  282.2 7.8 %broadcast_multiply_fusion = f32[8,2,2,5,8192]{4,3,2,1,0:T(8,128)} fusion(f32[8,2,2,5,8192]{4,3,2,1,0:T(8,128)} %reshape.193, f32[8192]{0:T(1024)S(1)} %sqrt.3), kind=kLoop, calls=%fused_computation.2 | loop fusion | flops 1310720 | bytes 10518528 | tf_op jit(solution)/shard_map/mul | solution.py:55
  290.0 9.8 %copy.19 = f32[8,2,2,5,8192]{4,2,3,1,0:T(2,128)} copy(f32[8,2,2,5,8192]{4,3,2,1,0:T(8,128)} %broadcast_multiply_fusion) | data formatting | bytes 10485760
  (9 shorter events, 0.1 us)
Async XLA Ops:
  7.2 217.6 %reduce-scatter.2.cloned.1.call-start = ((), (), s32[]{:S(2)}) async-start(), calls=%async_computation.1 | async-start | bytes 26214400 | tf_op jit(solution)/shard_map/reduce_scatter | solution.py:48
  34.9 0.8 copy-start
Sparse Core Ops, SparseCore 0:
  35.1 189.6 reduce-scatter.1
where the time goes:
time: 308 us; the launch traced here: 307 us
  waiting for transfers between devices  189 us (61%)
  matrix products  39.8 us (13%)
  local copies, waits for them, and re-layouts  37.3 us (12%)
  blocking collectives  17.6 us (6%)
  between operations  14.1 us (5%)
  other arithmetic  8.87 us (3%)
    reduce_scatter x1, waiting for transfers between devices, on_device(): lax.psum_scatter(jnp.dot(rotation_multipliers, flat_snapshots, preferred_...  189 us
    dot_general x1, matrix products, gram_terms(): jnp.einsum('fam,fbm->fab', flat, flat, precision=lax.Precision.HIGHEST)  25.9 us
    unnamed x5, local copies, waits for them, and re-layouts  23.9 us
    psum x1, blocking collectives, on_device(): summed = lax.psum(gram_terms(spectra), ('px', 'py'))  17.6 us
    dot_general x1, matrix products, on_device(): jnp.dot(rotation_multipliers, flat_snapshots, preferred_element_type=jnp....  13.8 us
    reshape x2, local copies, waits for them, and re-layouts, on_device(): raw.reshape(RETAINED_MODES // groups, SEGMENT_NUMBER, 2, VARS, point_count)  13.2 us
    mul x1, other arithmetic, on_device(): spectra = raw * jnp.sqrt(quad_weights)  7.76 us
  transfers between devices with their start and end apart: 1, of which 1 were waited for; matrix products, arithmetic and copies ran while one was open for 0% of the time, Pallas kernels for 0%

commit v1 on v0

--- a/solution.py
+++ b/solution.py
@@ -53,7 +53,7 @@
     )
     raw = raw.reshape(RETAINED_MODES // groups, SEGMENT_NUMBER, 2, VARS, point_count)
     spectra = raw * jnp.sqrt(quad_weights)
-    summed = lax.psum(gram_terms(spectra), ("px", "py"))
+    summed = jax.lax.psum(jax.lax.psum(gram_terms(spectra), "py"), "px")
     total_points = point_count * lax.axis_size("px") * lax.axis_size("py")
     gram = summed / jnp.float32(total_points * VARS)
     return (spectra, gram)

time: 308 us -> 305 us (level)
    psum x1 -> x2, blocking collectives: 17.6 us -> 14.7 us  [on_device(): summed = jax.lax.psum(jax.lax.psum(gram_terms(spectra), 'py'), 'px')]
where the time goes in v1:
time: 305 us; the launch traced here: 304 us
  waiting for transfers between devices  189 us (62%)
  matrix products  39.8 us (13%)
  local copies, waits for them, and re-layouts  37.3 us (12%)
  blocking collectives  14.7 us (5%)
  between operations  14.1 us (5%)
  other arithmetic  8.88 us (3%)
    reduce_scatter x1, waiting for transfers between devices, on_device(): lax.psum_scatter(jnp.dot(rotation_multipliers, flat_snapshots, preferred_...  189 us
    dot_general x1, matrix products, gram_terms(): jnp.einsum('fam,fbm->fab', flat, flat, precision=lax.Precision.HIGHEST)  25.9 us
    unnamed x5, local copies, waits for them, and re-layouts  23.9 us
    psum x2, blocking collectives, on_device(): summed = jax.lax.psum(jax.lax.psum(gram_terms(spectra), 'py'), 'px')  14.7 us
    dot_general x1, matrix products, on_device(): jnp.dot(rotation_multipliers, flat_snapshots, preferred_element_type=jnp....  13.8 us
    reshape x2, local copies, waits for them, and re-layouts, on_device(): raw.reshape(RETAINED_MODES // groups, SEGMENT_NUMBER, 2, VARS, point_count)  13.2 us
    mul x1, other arithmetic, on_device(): spectra = raw * jnp.sqrt(quad_weights)  7.77 us
  transfers between devices with their start and end apart: 1, of which 1 were waited for; matrix products, arithmetic and copies ran while one was open for 0% of the time, Pallas kernels for 0%

profile of v1, /device:TPU:1, one launch (start us, length us, event | category | flops | bytes accessed | tf_op | source)
XLA Modules:
  0.0 303.7 jit_solution(4045065501944685693)
XLA Ops:
  7.2 0.0 reduce-scatter.2.cloned.1.call-start
  7.2 0.1 broadcast_subtract_fusion
  7.3 0.1 fusion.6
  7.4 0.9 multiply_convert_fusion.1
  8.4 12.7 %copy.17 = bf16[96,5,8192]{0,2,1:T(8,128)(2,1)} copy(bf16[96,5,8192]{2,0,1:T(8,128)(2,1)} %param.3) | data formatting | bytes 15728640 | tf_op args[0]
  21.1 13.8 %fusion.7 = f32[128,40960]{1,0:T(8,128)} fusion(bf16[128,96]{1,0:T(8,128)(2,1)S(1)} %bitcast.8, bf16[96,40960]{0,1:T(8,128)(2,1)} %bitcast.7), kind=kOutput, calls=%fused_computation.24 | convolution fusion | flops 1006632960 | bytes 28860416 | tf_op jit(solution)/shard_map/dot_general | solution.py:49
  34.9 0.0 copy-start
  34.9 0.0 reduce-scatter.2.cloned.1.call-update
  34.9 0.7 copy-done
  35.7 0.1 mul.103
  35.8 188.9 %reduce-scatter.2.cloned.1.call-done = f32[32,40960]{1,0:T(8,128)} async-done(((f32[128,40960]{1,0:T(8,128)}), f32[32,40960]{1,0:T(8,128)}) %reduce-scatter.2.cloned.1.call-update) | async-done | bytes 5242896 | tf_op jit(solution)/shard_map/reduce_scatter | solution.py:48
  224.7 5.8 %reshape.194 = f32[8,4,40960]{2,1,0:T(4,128)} reshape(f32[32,40960]{1,0:T(8,128)} %reduce-scatter.2.cloned.1.call-done) | data formatting | bytes 10485760 | tf_op jit(solution)/shard_map/reshape | solution.py:54
  230.6 25.9 %fusion = f32[8,4,4]{2,1,0:T(4,128)S(1)} fusion(f32[8,4,40960]{2,1,0:T(4,128)} %reshape.194, f32[40960]{0:T(1024)S(1)} %mul.103), kind=kOutput, calls=%fused_computation | convolution fusion | flops 64225280 | bytes 5407232 | tf_op jit(solution)/shard_map/fam,fbm->fab/dot_general | solution.py:32
  256.5 0.1 copy.18
  256.7 9.7 %psum.14 = f32[8,2,2,2]{0,2,3,1:T(2,128)S(1)} all-reduce(f32[8,2,2,2]{0,2,3,1:T(2,128)S(1)} %pad_maximum_fusion.1), channel_id=1, replica_groups=mesh['px'=2,'py'=4,'ta'=4] {'py'}, use_global_device_ids=true, to_apply=%region_1.2 | all-reduce | flops 64 | bytes 512 | tf_op jit(solution)/shard_map/psum | solution.py:56
  266.3 5.0 %psum.15 = f32[8,2,2,2]{0,2,3,1:T(2,128)S(1)} all-reduce(f32[8,2,2,2]{0,2,3,1:T(2,128)S(1)} %psum.14), channel_id=1, replica_groups=mesh['px'=2,'py'=4,'ta'=4] {'px'}, use_global_device_ids=true, to_apply=%region_2.3 | all-reduce | flops 64 | bytes 512 | tf_op jit(solution)/shard_map/psum | solution.py:56
  271.3 0.6 copy.20
  271.9 7.3 %reshape.193 = f32[8,2,2,5,8192]{4,3,2,1,0:T(8,128)} reshape(f32[32,40960]{1,0:T(8,128)} %reduce-scatter.2.cloned.1.call-done) | data formatting | bytes 10485760 | tf_op jit(solution)/shard_map/reshape | solution.py:54
  279.3 7.8 %broadcast_multiply_fusion = f32[8,2,2,5,8192]{4,3,2,1,0:T(8,128)} fusion(f32[8,2,2,5,8192]{4,3,2,1,0:T(8,128)} %reshape.193, f32[8192]{0:T(1024)S(1)} %sqrt.3), kind=kLoop, calls=%fused_computation.2 | loop fusion | flops 1310720 | bytes 10518528 | tf_op jit(solution)/shard_map/mul | solution.py:55
  287.0 9.8 %copy.19 = f32[8,2,2,5,8192]{4,2,3,1,0:T(2,128)} copy(f32[8,2,2,5,8192]{4,3,2,1,0:T(8,128)} %broadcast_multiply_fusion) | data formatting | bytes 10485760
  (9 shorter events, 0.1 us)
Async XLA Ops:
  7.2 217.6 %reduce-scatter.2.cloned.1.call-start = ((), (), s32[]{:S(2)}) async-start(), calls=%async_computation.1 | async-start | bytes 26214400 | tf_op jit(solution)/shard_map/reduce_scatter | solution.py:48
  34.9 0.8 copy-start
Sparse Core Ops, SparseCore 0:
  35.1 189.6 reduce-scatter.1
